TPU v7x, 8 devices: a whole 2x2x1 slice. The times are simulated.
8 devices in a mesh: dp: 2 (over z, y), col: 2 (over x), fsdp: 2 (over core).
Axes of the slice: x: 2, y: 2, z: 1, core: 2. Of those that a mesh axis runs over, the one named last changes fastest.
Arguments:
- x_act: bfloat16 [32768, 576], P(('dp', 'col', 'fsdp'))
- dy_out: bfloat16 [32768, 576], P(('dp', 'col', 'fsdp'))
- w_gate: bfloat16 [576, 1536], P(None, ('col', 'fsdp'))
- w_up: bfloat16 [576, 1536], P(None, ('col', 'fsdp'))
- w_down: bfloat16 [1536, 576], P(('col', 'fsdp'))
- v_gate: bfloat16 [576, 1536], P(None, ('col', 'fsdp'))
- v_up: bfloat16 [576, 1536], P(None, ('col', 'fsdp'))
- v_down: bfloat16 [1536, 576], P(('col', 'fsdp'))
- g_next: float32 [8, 3, 576, 1536], P(('dp', 'col', 'fsdp'))
Outputs:
- output 1: bfloat16 [32768, 576], P(('dp', 'col', 'fsdp'))
- output 2: float32 [3, 576, 1536], P(None, None, ('col', 'fsdp'))
- output 3: float32 [8, 3, 576, 1536], P(('dp', 'col', 'fsdp'))
- output 4: bfloat16 [576, 1536], replicated
- output 5: bfloat16 [576, 1536], replicated
- output 6: bfloat16 [1536, 576], replicated
All inputs are finite; a program needn't handle non-finite values.
Results may differ from a plain program's by a relative error of at most 0.00911928.
Values are sent between devices in bfloat16 or wider.
A program may use at most 1 GiB of HBM per device.

v0:
```python
import jax
import jax.numpy as jnp
from jax import lax
from jax.sharding import PartitionSpec as P

ALL_AXES = ('dp', 'col', 'fsdp')
FSDP_AXES = ('col', 'fsdp')


def local_backward(x_loc, dy_loc, gate_full, up_full, down_full):
    pre_gate = jnp.dot(x_loc, gate_full, preferred_element_type=jnp.float32)
    pre_up = jnp.dot(x_loc, up_full, preferred_element_type=jnp.float32)
    sig_gate = jax.nn.sigmoid(pre_gate)
    act_gate = pre_gate * sig_gate
    hidden = (act_gate * pre_up).astype(jnp.bfloat16)
    d_hidden = jnp.einsum('td,fd->tf', dy_loc, down_full, preferred_element_type=jnp.float32)
    d_gate = (d_hidden * pre_up * sig_gate * (1.0 + pre_gate * (1.0 - sig_gate))).astype(jnp.bfloat16)
    d_up = (d_hidden * act_gate).astype(jnp.bfloat16)
    dx_loc = (jnp.einsum('tf,df->td', d_gate, gate_full, preferred_element_type=jnp.float32)
              + jnp.einsum('tf,df->td', d_up, up_full, preferred_element_type=jnp.float32)).astype(jnp.bfloat16)
    grad_local = jnp.stack([
        jnp.einsum('td,tf->df', x_loc, d_gate, preferred_element_type=jnp.float32),
        jnp.einsum('td,tf->df', x_loc, d_up, preferred_element_type=jnp.float32),
        jnp.einsum('td,tf->df', dy_loc, hidden, preferred_element_type=jnp.float32),
    ])
    return dx_loc, grad_local


def solution(mesh):
    def device_step(x_loc, dy_loc, w_gate, w_up, w_down, v_gate, v_up, v_down, g_next):
        gate_full = lax.all_gather(w_gate, FSDP_AXES, axis=1, tiled=True)
        up_full = lax.all_gather(w_up, FSDP_AXES, axis=1, tiled=True)
        down_full = lax.all_gather(w_down, FSDP_AXES, axis=0, tiled=True)
        v_gate_full = lax.all_gather(v_gate, FSDP_AXES, axis=1, tiled=True)
        v_up_full = lax.all_gather(v_up, FSDP_AXES, axis=1, tiled=True)
        v_down_full = lax.all_gather(v_down, FSDP_AXES, axis=0, tiled=True)
        grad_shard = lax.psum_scatter(g_next[0].astype(jnp.bfloat16), FSDP_AXES, scatter_dimension=2, tiled=True)
        grad_next = lax.psum(grad_shard.astype(jnp.float32), 'dp')
        dx_loc, grad_local = local_backward(x_loc, dy_loc, gate_full, up_full, down_full)
        return dx_loc, grad_next, grad_local[None], v_gate_full, v_up_full, v_down_full

    row_spec = P(ALL_AXES, None)
    col_shard = P(None, FSDP_AXES)
    row_shard = P(FSDP_AXES, None)
    dev_spec = P(ALL_AXES, None, None, None)
    return jax.shard_map(
        device_step, mesh=mesh,
        in_specs=(row_spec, row_spec, col_shard, col_shard, row_shard, col_shard, col_shard, row_shard, dev_spec),
        out_specs=(row_spec, P(None, None, FSDP_AXES), dev_spec, P(), P(), P()),
        check_vma=False)
```

profile of v0, /device:TPU:0, one launch (start us, length us, event | category | flops | bytes accessed | tf_op | source)
XLA Modules:
  0.0 277.0 jit_solution(8360970767839811148)
XLA Ops:
  7.2 0.0 all-gather.9.cloned.1.call-start
  7.2 0.7 all-gather.9.cloned.1.call-update
  7.9 0.0 all-gather.11.cloned.1.call-start
  7.9 0.7 all-gather.11.cloned.1.call-update
  8.6 0.0 all-gather.7.cloned.1.call-start
  8.7 0.7 all-gather.7.cloned.1.call-update
  9.4 0.0 all-gather.13.cloned.1.call-start
  9.4 0.5 all-gather.13.cloned.1.call-update
  10.0 0.0 all-gather.15.cloned.1.call-start
  10.0 0.5 all-gather.15.cloned.1.call-update
  10.5 0.0 all-gather.17.cloned.1.call-start
  10.6 0.5 all-gather.17.cloned.1.call-update
  11.1 0.0 reduce-scatter.4.cloned.1.call-start
  11.2 7.0 %convert_bitcast_fusion = bf16[3,576,1536]{2,1,0:T(8,128)(2,1)} fusion(f32[1,3,576,1536]{3,2,1,0:T(8,128)} %param.17), kind=kLoop, calls=%fused_computation.8 | loop fusion | flops 2654208 | bytes 15925248 | tf_op jit(solution)/shard_map/convert_element_type | solution.py:37
  18.2 12.5 %copy.15 = bf16[3,576,1536]{1,0,2:T(4,128)(2,1)} copy(bf16[3,576,1536]{2,1,0:T(8,128)(2,1)} %convert_bitcast_fusion) | data formatting | bytes 10616832
  30.7 15.8 %reshape.13 = bf16[1536,1728]{1,0:T(8,128)(2,1)} reshape(bf16[1536,3,576]{2,1,0:T(4,128)(2,1)} %bitcast.33) | data formatting | bytes 10616832
  46.5 0.0 reduce-scatter.4.cloned.1.call-update
  46.5 0.0 all-gather.9.cloned.1.call-done
  46.6 16.9 %fusion.5 = f32[4096,1536]{1,0:T(8,128)} fusion(bf16[4096,576]{0,1:T(8,128)(2,1)} %param.9, bf16[576,1536]{1,0:T(8,128)(2,1)} %all-gather.9.cloned.1.call-done), kind=kOutput, calls=%fused_computation.13 | convolution fusion | flops 7247757312 | bytes 31653888 | tf_op jit(solution)/shard_map/dot_general | solution.py:12
  63.5 0.0 all-gather.11.cloned.1.call-done
  63.5 16.9 %fusion.6 = f32[4096,1536]{1,0:T(8,128)} fusion(bf16[4096,576]{0,1:T(8,128)(2,1)} %param.9, bf16[576,1536]{1,0:T(8,128)(2,1)} %all-gather.11.cloned.1.call-done), kind=kOutput, calls=%fused_computation.14 | convolution fusion | flops 7247757312 | bytes 31653888 | tf_op jit(solution)/shard_map/dot_general | solution.py:11
  80.4 0.0 all-gather.7.cloned.1.call-done
  80.4 33.8 %multiply_convert_fusion.1 = (bf16[4096,1536]{1,0:T(8,128)(2,1)}, bf16[4096,1536]{1,0:T(8,128)(2,1)}) fusion(f32[4096,1536]{1,0:T(8,128)} %fusion.6, f32[4096,1536]{1,0:T(8,128)} %fusion.5, bf16[4096,576]{0,1:T(8,128)(2,1)} %param.10, bf16[1536,576]{0,1:T(8,128)(2,1)} %all-gather.7.cloned.1.call-done), kind=kOutput, calls=%fused_computation.1 | convolution fusion | flops 7329546240 | bytes 81985536 | tf_op jit(solution)/shard_map/td,fd->tf/dot_general | solution.py:16
  114.2 11.5 %convolution_bitcast_fusion = f32[1,576,1536]{2,1,0:T(8,128)S(1)} fusion(bf16[4096,576]{0,1:T(8,128)(2,1)} %param.9, bf16[4096,1536]{1,0:T(8,128)(2,1)} %get-tuple-element.6), kind=kOutput, calls=%fused_computation.10 | convolution fusion | flops 7247757312 | bytes 20840448 | tf_op jit(solution)/shard_map/td,tf->df/dot_general | solution.py:23
  125.7 0.0 all-gather.13.cloned.1.call-done
  125.7 0.0 all-gather.15.cloned.1.call-done
  125.8 0.2 all-gather.17.cloned.1.call-done
  126.0 11.5 %convolution_bitcast_fusion.1 = f32[1,576,1536]{2,1,0:T(8,128)S(1)} fusion(bf16[4096,576]{0,1:T(8,128)(2,1)} %param.9, bf16[4096,1536]{1,0:T(8,128)(2,1)} %get-tuple-element.7), kind=kOutput, calls=%fused_computation.11 | convolution fusion | flops 7247757312 | bytes 20840448 | tf_op jit(solution)/shard_map/td,tf->df/dot_general | solution.py:22
  137.4 19.7 %fusion.3 = f32[1,576,1536]{2,1,0:T(8,128)S(1)} fusion(bf16[4096,576]{0,1:T(8,128)(2,1)} %param.10, f32[4096,1536]{1,0:T(8,128)} %fusion.5, f32[4096,1536]{1,0:T(8,128)} %fusion.6), kind=kOutput, calls=%fused_computation.9 | convolution fusion | flops 7285506048 | bytes 58589184 | tf_op jit(solution)/shard_map/td,tf->df/dot_general | solution.py:24
  157.2 0.0 copy-start.3
  157.2 5.3 %maximum_bitcast_fusion = f32[1,3,576,1536]{3,2,1,0:T(8,128)} fusion(f32[1,576,1536]{2,1,0:T(8,128)S(1)} %fusion.3, f32[1,576,1536]{2,1,0:T(8,128)S(1)} %convolution_bitcast_fusion, f32[1,576,1536]{2,1,0:T(8,128)S(1)} %convolution_bitcast_fusion.1), kind=kLoop, calls=%fused_computation.6 | loop fusion | flops 5308416 | bytes 21233664 | tf_op jit(solution)/shard_map/broadcast_in_dim | solution.py:40
  162.4 0.0 copy-done.3
  162.4 0.0 copy-start.2
  162.4 10.6 %fusion.7 = f32[4096,576]{0,1:T(8,128)S(1)} fusion(bf16[4096,1536]{1,0:T(8,128)(2,1)} %get-tuple-element.7, bf16[576,1536]{1,0:T(8,128)(2,1)S(1)} %copy-done.3), kind=kOutput, calls=%fused_computation.15 | convolution fusion | flops 7247757312 | bytes 23789568 | tf_op jit(solution)/shard_map/tf,df->td/dot_general | solution.py:19
  173.1 0.0 copy-done.2
  173.1 18.4 %add_convert_fusion = bf16[4096,576]{0,1:T(8,128)(2,1)} fusion(f32[4096,576]{0,1:T(8,128)S(1)} %fusion.7, bf16[4096,1536]{1,0:T(8,128)(2,1)} %get-tuple-element.6, bf16[576,1536]{1,0:T(8,128)(2,1)S(1)} %copy-done.2), kind=kOutput, calls=%fused_computation.7 | convolution fusion | flops 7252475904 | bytes 28508160 | tf_op jit(solution)/shard_map/tf,df->td/dot_general | solution.py:20
  191.5 0.0 reduce-scatter.4.cloned.1.call-done
  191.5 4.0 %reshape.14 = bf16[384,3,576]{2,1,0:T(4,128)(2,1)S(1)} reshape(bf16[384,1728]{1,0:T(8,128)(2,1)} %reduce-scatter.4.cloned.1.call-done) | data formatting | bytes 2654208
  195.4 2.1 copy.16
  197.6 0.0 copy-start
  197.6 67.3 %all-reduce.1 = f32[3,576,384]{2,1,0:T(8,128)} all-reduce(bf16[3,576,384]{2,1,0:T(8,128)(2,1)S(1)} %copy.16), channel_id=1, replica_groups=mesh['dp'=2,'col'=2,'fsdp'=2] {'dp'}, use_global_device_ids=true, to_apply=%region_1.0 | all-reduce | flops 663552 | bytes 3981312 | tf_op jit(solution)/shard_map/psum | solution.py:38
  264.8 0.0 copy-start.1
  264.8 2.9 %copy.22 = bf16[576,1536]{1,0:T(8,128)(2,1)} copy(bf16[576,1536]{1,0:T(8,128)(2,1)} %all-gather.13.cloned.1.call-done) | data formatting | bytes 3538944
  267.7 0.0 copy-done
  267.8 1.2 copy.23
  269.0 0.0 copy-done.1
  269.0 1.2 copy.24
Async XLA Ops:
  7.2 39.4 %all-gather.9.cloned.1.call-start = ((), (), s32[]{:S(2)}) async-start(), calls=%async_computation.2 | async-start | bytes 2211840 | tf_op jit(solution)/shard_map/all_gather | solution.py:32
  7.9 55.6 %all-gather.11.cloned.1.call-start = ((), (), s32[]{:S(2)}) async-start(), calls=%async_computation.3 | async-start | bytes 2211840 | tf_op jit(solution)/shard_map/all_gather | solution.py:31
  8.6 71.8 %all-gather.7.cloned.1.call-start = ((), (), s32[]{:S(2)}) async-start(), calls=%async_computation.1 | async-start | bytes 2211840 | tf_op jit(solution)/shard_map/all_gather | solution.py:33
  9.4 116.3 %all-gather.13.cloned.1.call-start = ((), (), s32[]{:S(2)}) async-start(), calls=%async_computation.4 | async-start | bytes 2211840 | tf_op jit(solution)/shard_map/all_gather | solution.py:34
  10.0 115.8 %all-gather.15.cloned.1.call-start = ((), (), s32[]{:S(2)}) async-start(), calls=%async_computation.5 | async-start | bytes 2211840 | tf_op jit(solution)/shard_map/all_gather | solution.py:35
  10.5 115.4 %all-gather.17.cloned.1.call-start = ((), (), s32[]{:S(2)}) async-start(), calls=%async_computation.6 | async-start | bytes 2211840 | tf_op jit(solution)/shard_map/all_gather | solution.py:36
  11.1 180.3 %reduce-scatter.4.cloned.1.call-start = ((), (), s32[]{:S(2)}) async-start(), calls=%async_computation.7 | async-start | bytes 6881280
  157.2 5.3 %copy-start.3 = (bf16[576,1536]{1,0:T(8,128)(2,1)S(1)}, bf16[576,1536]{1,0:T(8,128)(2,1)}, u32[]{:S(2)}) copy-start(bf16[576,1536]{1,0:T(8,128)(2,1)} %all-gather.11.cloned.1.call-done) | copy-start | bytes 5308420
  162.4 10.6 %copy-start.2 = (bf16[576,1536]{1,0:T(8,128)(2,1)S(1)}, bf16[576,1536]{1,0:T(8,128)(2,1)}, u32[]{:S(2)}) copy-start(bf16[576,1536]{1,0:T(8,128)(2,1)} %all-gather.9.cloned.1.call-done) | copy-start | bytes 5308420
  197.6 70.2 %copy-start = (bf16[576,1536]{1,0:T(8,128)(2,1)S(1)}, bf16[576,1536]{1,0:T(8,128)(2,1)}, u32[]{:S(2)}) copy-start(bf16[576,1536]{1,0:T(8,128)(2,1)} %all-gather.15.cloned.1.call-done) | copy-start | bytes 5308420
  264.8 4.1 %copy-start.1 = (bf16[1536,576]{0,1:T(8,128)(2,1)S(1)}, bf16[1536,576]{0,1:T(8,128)(2,1)}, u32[]{:S(2)}) copy-start(bf16[1536,576]{0,1:T(8,128)(2,1)} %all-gather.17.cloned.1.call-done) | copy-start | bytes 5308420
Sparse Core Ops, SparseCore 0:
  9.5 20.5 all-gather.8
  31.6 17.6 all-gather.10
  50.9 17.6 all-gather.6
  70.0 17.6 all-gather.12
  89.1 17.6 all-gather.14
  108.2 17.6 all-gather.16
  128.4 46.4 reduce-scatter.3
where the time goes:
time: 278 us; the launch traced here: 277 us
  matrix products  139 us (50%)
  blocking collectives  67.3 us (24%)
  local copies, waits for them, and re-layouts  39.7 us (14%)
  between operations  14.2 us (5%)
  other arithmetic  12.3 us (4%)
  waiting for transfers between devices  3.91 us (1%)
    psum x1, blocking collectives, device_step(): grad_next = lax.psum(grad_shard.astype(jnp.float32), 'dp')  67.3 us
    unnamed x15, local copies, waits for them, and re-layouts  39.7 us
    dot_general x1, matrix products, local_backward(): jnp.einsum('td,fd->tf', dy_loc, down_full, preferred_element_type=jnp.flo...  33.8 us
    dot_general x1, matrix products, local_backward(): jnp.einsum('td,tf->df', dy_loc, hidden, preferred_element_type=jnp.float32)  19.7 us
    dot_general x1, matrix products, local_backward(): jnp.einsum('tf,df->td', d_up, up_full, preferred_element_type=jnp.float32)  18.4 us
    dot_general x1, matrix products, local_backward(): pre_gate = jnp.dot(x_loc, gate_full, preferred_element_type=jnp.float32)  16.9 us
    dot_general x1, matrix products, local_backward(): pre_up = jnp.dot(x_loc, up_full, preferred_element_type=jnp.float32)  16.9 us
    dot_general x1, matrix products, local_backward(): jnp.einsum('td,tf->df', x_loc, d_gate, preferred_element_type=jnp.float32)  11.5 us
  transfers between devices with their start and end apart: 7, of which 1 were waited for; matrix products, arithmetic and copies ran while one was open for 65% of the time, Pallas kernels for 0%

commit v1 on v0

v1 whole, which is shorter than its diff:
```python
import functools
import jax
import jax.numpy as jnp
from jax import lax
from jax.experimental import pallas as pl
from jax.experimental.pallas import tpu as pltpu
from jax.sharding import PartitionSpec as P

ALL_AXES = ('dp', 'col', 'fsdp')
FSDP_AXES = ('col', 'fsdp')
D, F, T = 576, 1536, 4096
FH = F // 2
TT = 512
NT = T // TT
F32, BF16 = jnp.float32, jnp.bfloat16


def dot(a, b, ca, cb):
    return lax.dot_general(a, b, (((ca,), (cb,)), ((), ())), preferred_element_type=F32)


def tile_step(i, first, x_ref, dy_ref, w13, w2, dxt, dw13, dw2):
    x, dy = x_ref[i], dy_ref[i]
    ab = dot(x, w13[...], 1, 0)
    dh = dot(dy, w2[...], 1, 1)
    a, b = ab[:, :FH], ab[:, FH:]
    s = 0.5 * jnp.tanh(0.5 * a) + 0.5
    act = a * s
    h = (act * b).astype(BF16)
    dg = (dh * b * s * (1.0 + a * (1.0 - s))).astype(BF16)
    du = (dh * act).astype(BF16)
    dgu = jnp.concatenate([dg, du], axis=1)
    dxt_new = dot(w13[...], dgu, 1, 1)
    if first:
        dxt[i] = dxt_new
    else:
        dxt[i] = dxt[i] + dxt_new
    dw13[...] += dot(x, dgu, 0, 0)
    dw2[...] += dot(dy, h, 0, 0)


def kernel(x_hbm, dy_hbm, w1, w3, w2, dx_hbm, dw_hbm, xv, dyv, w13v, w2v, dxt, dw13, dw2, dxo, sems, osem):
    cx = pltpu.make_async_copy(x_hbm, xv, sems.at[0])
    cy = pltpu.make_async_copy(dy_hbm, dyv, sems.at[1])
    cx.start()
    cy.start()
    cx.wait()
    cy.wait()
    for p in range(2):
        lo = p * FH
        cw = [pltpu.make_async_copy(w1.at[:, pl.ds(lo, FH)], w13v.at[:, pl.ds(0, FH)], sems.at[2]),
              pltpu.make_async_copy(w3.at[:, pl.ds(lo, FH)], w13v.at[:, pl.ds(FH, FH)], sems.at[3]),
              pltpu.make_async_copy(w2.at[pl.ds(lo, FH), :], w2v, sems.at[4])]
        for c in cw:
            c.start()
        for c in cw:
            c.wait()
        dw13[...] = jnp.zeros_like(dw13)
        dw2[...] = jnp.zeros_like(dw2)

        @pl.loop(0, NT)
        def _(i):
            tile_step(i, p == 0, xv, dyv, w13v, w2v, dxt, dw13, dw2)
            if p == 1:
                @pl.when(i > 0)
                def _():
                    pltpu.make_async_copy(dxo, dx_hbm.at[i - 1], osem).wait()
                dxo[...] = dxt[i].astype(BF16).T
                pltpu.make_async_copy(dxo, dx_hbm.at[i], osem).start()
        co = [pltpu.make_async_copy(dw13.at[:, pl.ds(0, FH)], dw_hbm.at[0, :, pl.ds(lo, FH)], sems.at[2]),
              pltpu.make_async_copy(dw13.at[:, pl.ds(FH, FH)], dw_hbm.at[1, :, pl.ds(lo, FH)], sems.at[3]),
              pltpu.make_async_copy(dw2, dw_hbm.at[2, :, pl.ds(lo, FH)], sems.at[4])]
        for c in co:
            c.start()
        for c in co:
            c.wait()
    pltpu.make_async_copy(dxo, dx_hbm.at[NT - 1], osem).wait()


def mlp(x, dy, w1, w3, w2):
    anys = pl.BlockSpec(memory_space=pl.ANY)
    dx, dw = pl.pallas_call(
        kernel,
        out_shape=[jax.ShapeDtypeStruct((NT, TT, D), BF16), jax.ShapeDtypeStruct((3, D, F), F32)],
        in_specs=[anys] * 5, out_specs=[anys] * 2,
        scratch_shapes=[
            pltpu.VMEM((NT, TT, D), BF16), pltpu.VMEM((NT, TT, D), BF16),
            pltpu.VMEM((D, F), BF16), pltpu.VMEM((FH, D), BF16),
            pltpu.VMEM((NT, D, TT), F32), pltpu.VMEM((D, F), F32), pltpu.VMEM((D, FH), F32),
            pltpu.VMEM((TT, D), BF16),
            pltpu.SemaphoreType.DMA((5,)), pltpu.SemaphoreType.DMA,
        ],
        compiler_params=pltpu.CompilerParams(vmem_limit_bytes=67043328),
        cost_estimate=pl.CostEstimate(flops=8 * 2 * T * D * F, bytes_accessed=40 * 2**20, transcendentals=T * F),
        name='mlp_bwd',
    )(x.reshape(NT, TT, D), dy.reshape(NT, TT, D), w1, w3, w2)
    return dx.reshape(T, D), dw


def solution(mesh):
    def device_step(x_loc, dy_loc, w_gate, w_up, w_down, v_gate, v_up, v_down, g_next):
        gate_full = lax.all_gather(w_gate, FSDP_AXES, axis=1, tiled=True)
        up_full = lax.all_gather(w_up, FSDP_AXES, axis=1, tiled=True)
        down_full = lax.all_gather(w_down, FSDP_AXES, axis=0, tiled=True)
        v_gate_full = lax.all_gather(v_gate, FSDP_AXES, axis=1, tiled=True)
        v_up_full = lax.all_gather(v_up, FSDP_AXES, axis=1, tiled=True)
        v_down_full = lax.all_gather(v_down, FSDP_AXES, axis=0, tiled=True)
        grad_shard = lax.psum_scatter(g_next[0].astype(jnp.bfloat16), FSDP_AXES, scatter_dimension=2, tiled=True)
        other = lax.ppermute(grad_shard, 'dp', [(0, 1), (1, 0)])
        grad_next = grad_shard.astype(F32) + other.astype(F32)
        dx_loc, grad_local = mlp(x_loc, dy_loc, gate_full, up_full, down_full)
        return dx_loc, grad_next, grad_local[None], v_gate_full, v_up_full, v_down_full

    row_spec = P(ALL_AXES, None)
    col_shard = P(None, FSDP_AXES)
    row_shard = P(FSDP_AXES, None)
    dev_spec = P(ALL_AXES, None, None, None)
    return jax.shard_map(
        device_step, mesh=mesh,
        in_specs=(row_spec, row_spec, col_shard, col_shard, row_shard, col_shard, col_shard, row_shard, dev_spec),
        out_specs=(row_spec, P(None, None, FSDP_AXES), dev_spec, P(), P(), P()),
        check_vma=False)
```

time: 278 us -> 261 us (0.939)
  matrix products: 139 us -> 0 us
  Pallas kernels: 0 us -> 84.8 us
  waiting for transfers between devices: 3.91 us -> 83.6 us
  blocking collectives: 67.3 us -> 0 us
  local copies, waits for them, and re-layouts: 39.7 us -> 64.8 us
    dot_general x8 -> x0, matrix products: 139 us -> none  [the longest x1 33.8 us: local_backward(): jnp.einsum('td,fd->tf', dy_loc, down_full, preferred_element_type=jnp.flo...]
    pallas_call x0 -> x1, Pallas kernels: none -> 84.8 us  [mlp(): pl.pallas_call(kernel, out_shape=[jax.ShapeDtypeStruct((NT, TT, D), BF16)...]
    psum x1 -> x0, blocking collectives: 67.3 us -> none  [device_step(): grad_next = lax.psum(grad_shard.astype(jnp.float32), 'dp')]
    unnamed x8, waiting for transfers between devices: 3.65 us -> 32.8 us
    unnamed x15 -> x19, local copies, waits for them, and re-layouts: 39.7 us -> 64.8 us
    all_gather x1, waiting for transfers between devices: 0.01 us -> 20.8 us  [device_step(): down_full = lax.all_gather(w_down, FSDP_AXES, axis=0, tiled=True)]
    all_gather x1, waiting for transfers between devices: 0.02 us -> 19.3 us  [device_step(): up_full = lax.all_gather(w_up, FSDP_AXES, axis=1, tiled=True)]
    all_gather x1, waiting for transfers between devices: 0.01 us -> 10.7 us  [device_step(): gate_full = lax.all_gather(w_gate, FSDP_AXES, axis=1, tiled=True)]
  transfers between devices with their start and end apart: 7 -> 8, of which waited for: 1 -> 4; matrix products, arithmetic and copies ran while one was open for 65% -> 12% of each run, Pallas kernels for 0% -> 33%
where the time goes in v1:
time: 261 us; the launch traced here: 260 us
  Pallas kernels  84.8 us (32%)
  waiting for transfers between devices  83.6 us (32%)
  local copies, waits for them, and re-layouts  64.8 us (25%)
  between operations  14.2 us (5%)
  other arithmetic  10.6 us (4%)
    pallas_call x1, Pallas kernels, mlp(): pl.pallas_call(kernel, out_shape=[jax.ShapeDtypeStruct((NT, TT, D), BF16)...  84.8 us
    unnamed x19, local copies, waits for them, and re-layouts  64.8 us
    unnamed x8, waiting for transfers between devices  32.8 us
    all_gather x1, waiting for transfers between devices, device_step(): down_full = lax.all_gather(w_down, FSDP_AXES, axis=0, tiled=True)  20.8 us
    all_gather x1, waiting for transfers between devices, device_step(): up_full = lax.all_gather(w_up, FSDP_AXES, axis=1, tiled=True)  19.3 us
    all_gather x1, waiting for transfers between devices, device_step(): gate_full = lax.all_gather(w_gate, FSDP_AXES, axis=1, tiled=True)  10.7 us
    convert_element_type x1, other arithmetic, device_step(): g_next[0].astype(jnp.bfloat16)  7.03 us
  transfers between devices with their start and end apart: 8, of which 4 were waited for; matrix products, arithmetic and copies ran while one was open for 12% of the time, Pallas kernels for 33%

profile of v1, /device:TPU:0, one launch (start us, length us, event | category | flops | bytes accessed | tf_op | source)
XLA Modules:
  0.0 259.7 jit_solution(5586254750435072774)
XLA Ops:
  7.2 0.0 reduce-scatter.4.cloned.1.call-start
  7.2 7.0 %convert_bitcast_fusion = bf16[3,576,1536]{2,1,0:T(8,128)(2,1)} fusion(f32[1,3,576,1536]{3,2,1,0:T(8,128)} %param.17), kind=kLoop, calls=%fused_computation | loop fusion | flops 2654208 | bytes 15925248 | tf_op jit(solution)/shard_map/convert_element_type | solution.py:108
  14.2 12.5 %copy.23 = bf16[3,576,1536]{1,0,2:T(4,128)(2,1)} copy(bf16[3,576,1536]{2,1,0:T(8,128)(2,1)} %convert_bitcast_fusion) | data formatting | bytes 10616832
  26.7 15.8 %reshape.25 = bf16[1536,1728]{1,0:T(8,128)(2,1)} reshape(bf16[1536,3,576]{2,1,0:T(4,128)(2,1)} %bitcast.8) | data formatting | bytes 10616832
  42.5 0.0 copy-start.3
  42.5 0.0 reduce-scatter.4.cloned.1.call-update
  42.5 0.0 all-gather.7.cloned.1.call-start
  42.6 0.7 all-gather.7.cloned.1.call-update
  43.3 0.0 all-gather.9.cloned.1.call-start
  43.3 0.7 all-gather.9.cloned.1.call-update
  44.0 0.0 all-gather.11.cloned.1.call-start
  44.1 0.0 copy-done.3
  44.1 1.0 copy.21
  45.1 0.0 all-gather.11.cloned.1.call-update
  45.1 0.0 all-gather.13.cloned.1.call-start
  45.2 0.5 all-gather.13.cloned.1.call-update
  45.7 0.0 all-gather.15.cloned.1.call-start
  45.7 0.5 all-gather.15.cloned.1.call-update
  46.3 0.0 all-gather.17.cloned.1.call-start
  46.3 0.7 all-gather.17.cloned.1.call-update
  47.0 7.7 %copy.19 = bf16[4096,576]{1,0:T(8,128)(2,1)} copy(bf16[4096,576]{0,1:T(8,128)(2,1)} %param.9) | data formatting | bytes 9437184 | tf_op args[0]
  54.7 7.6 %copy.20 = bf16[4096,576]{1,0:T(8,128)(2,1)} copy(bf16[4096,576]{0,1:T(8,128)(2,1)} %param.10) | data formatting | bytes 9437184 | tf_op args[1]
  62.3 29.7 %reduce-scatter.4.cloned.1.call-done = bf16[384,1728]{1,0:T(8,128)(2,1)} async-done(((bf16[1536,1728]{1,0:T(8,128)(2,1)}), bf16[384,1728]{1,0:T(8,128)(2,1)}) %reduce-scatter.4.cloned.1.call-update) | async-done | bytes 1327120
  92.0 4.0 %reshape.26 = bf16[384,3,576]{2,1,0:T(4,128)(2,1)S(1)} reshape(bf16[384,1728]{1,0:T(8,128)(2,1)} %reduce-scatter.4.cloned.1.call-done) | data formatting | bytes 2654208
  95.9 3.2 %copy.24 = bf16[3,576,384]{2,1,0:T(8,128)(2,1)} copy(bf16[3,576,384]{1,0,2:T(4,128)(2,1)S(1)} %bitcast.9) | data formatting | bytes 2654208
  99.1 1.5 collective-permute-start
  100.6 10.7 %all-gather.7.cloned.1.call-done.w1 = bf16[576,1536]{1,0:T(8,128)(2,1)} async-done(((bf16[576,384]{1,0:T(8,128)(2,1)}), bf16[576,1536]{1,0:T(8,128)(2,1)}) %all-gather.7.cloned.1.call-update) | async-done | bytes 1769488 | tf_op jit(solution)/shard_map/all_gather | solution.py:102
  111.2 19.3 %all-gather.9.cloned.1.call-done.w3 = bf16[576,1536]{1,0:T(8,128)(2,1)} async-done(((bf16[576,384]{1,0:T(8,128)(2,1)}), bf16[576,1536]{1,0:T(8,128)(2,1)}) %all-gather.9.cloned.1.call-update) | async-done | bytes 1769488 | tf_op jit(solution)/shard_map/all_gather | solution.py:103
  130.5 20.8 %all-gather.11.cloned.1.call-done.w2 = bf16[1536,576]{1,0:T(8,128)(2,1)} async-done(((bf16[384,576]{1,0:T(8,128)(2,1)}), bf16[1536,576]{1,0:T(8,128)(2,1)}) %all-gather.11.cloned.1.call-update) | async-done | bytes 1769488 | tf_op jit(solution)/shard_map/all_gather | solution.py:104
  151.3 84.8 %mlp_bwd.1 = (bf16[8,512,576]{2,1,0:T(8,128)(2,1)}, f32[3,576,1536]{2,1,0:T(8,128)}) custom-call(bf16[8,512,576]{2,1,0:T(8,128)(2,1)} %bitcast.10, bf16[8,512,576]{2,1,0:T(8,128)(2,1)} %bitcast.11, bf16[576,1536]{1,0:T(8,128)(2,1)} %all-gather.7.cloned.1.call-done.w1, bf16[576,1536]{1,0:T(8,128)(2,1)} %all-gather.9.cloned.1.call-done.w3, ...), custom_call_target="tpu_custom_call" | custom-call | flops 57982058496 | bytes 41943040 | tf_op jit(solution)/shard_map/mlp_bwd/pallas_call | solution.py:82
  236.1 7.7 %copy.22 = bf16[4096,576]{0,1:T(8,128)(2,1)} copy(bf16[4096,576]{1,0:T(8,128)(2,1)} %bitcast.12) | data formatting | bytes 9437184
  243.8 0.0 all-gather.13.cloned.1.call-done
  243.8 0.0 copy-start
  243.8 0.0 all-gather.15.cloned.1.call-done
  243.8 0.0 all-gather.17.cloned.1.call-done
  243.8 0.0 collective-permute-done
  243.8 3.6 %convert_add_fusion = f32[3,576,384]{2,1,0:T(8,128)} fusion(bf16[3,576,384]{2,1,0:T(8,128)(2,1)} %collective-permute-done, bf16[3,576,384]{2,1,0:T(8,128)(2,1)} %copy.24), kind=kLoop, calls=%fused_computation.1 | loop fusion | flops 1990656 | bytes 5308416 | tf_op jit(solution)/shard_map/add | solution.py:110
  247.4 0.0 copy-start.1
  247.4 0.0 copy-done
  247.4 1.2 copy.28
  248.7 0.9 copy-done.1
  249.6 0.0 copy-start.2
  249.6 1.2 copy.29
  250.8 0.9 copy-done.2
  251.7 1.2 copy.30
Async XLA Ops:
  7.2 84.8 %reduce-scatter.4.cloned.1.call-start = ((), (), s32[]{:S(2)}) async-start(), calls=%async_computation.7 | async-start | bytes 6881280
  42.5 1.6 copy-start.3
  42.5 68.7 %all-gather.7.cloned.1.call-start = ((), (), s32[]{:S(2)}) async-start(), calls=%async_computation.1 | async-start | bytes 2211840 | tf_op jit(solution)/shard_map/all_gather | solution.py:102
  43.3 87.2 %all-gather.9.cloned.1.call-start = ((), (), s32[]{:S(2)}) async-start(), calls=%async_computation.2 | async-start | bytes 2211840 | tf_op jit(solution)/shard_map/all_gather | solution.py:103
  44.0 107.3 %all-gather.11.cloned.1.call-start = ((), (), s32[]{:S(2)}) async-start(), calls=%async_computation.3 | async-start | bytes 2457600 | tf_op jit(solution)/shard_map/all_gather | solution.py:104
  45.1 198.7 %all-gather.13.cloned.1.call-start = ((), (), s32[]{:S(2)}) async-start(), calls=%async_computation.4 | async-start | bytes 2211840 | tf_op jit(solution)/shard_map/all_gather | solution.py:105
  45.7 198.1 %all-gather.15.cloned.1.call-start = ((), (), s32[]{:S(2)}) async-start(), calls=%async_computation.5 | async-start | bytes 2211840 | tf_op jit(solution)/shard_map/all_gather | solution.py:106
  46.3 197.5 %all-gather.17.cloned.1.call-start = ((), (), s32[]{:S(2)}) async-start(), calls=%async_computation.6 | async-start | bytes 2211840 | tf_op jit(solution)/shard_map/all_gather | solution.py:107
  99.1 144.7 %collective-permute-start = (bf16[3,576,384]{2,1,0:T(8,128)(2,1)}, bf16[3,576,384]{2,1,0:T(8,128)(2,1)}, u32[]{:S(2)}, u32[]{:S(2)}) collective-permute-start(bf16[3,576,384]{2,1,0:T(8,128)(2,1)} %copy.24), channel_id=1, source_target_pairs={{0,4},{4,0},{1,5},{5,1},{2,6},{6,2},{3,7},{7,3}} | collective-permute-start | bytes 3981320 | tf_op jit(solution)/shard_map/ppermute | solution.py:109
  243.8 3.6 %copy-start = (bf16[576,1536]{1,0:T(8,128)(2,1)S(1)}, bf16[576,1536]{1,0:T(8,128)(2,1)}, u32[]{:S(2)}) copy-start(bf16[576,1536]{1,0:T(8,128)(2,1)} %all-gather.13.cloned.1.call-done) | copy-start | bytes 5308420
  247.4 2.1 copy-start.1
  249.6 2.1 copy-start.2
Sparse Core Ops, SparseCore 0:
  42.7 49.2 reduce-scatter.3
  93.5 17.6 all-gather.6
  112.8 17.6 all-gather.8
  132.5 18.7 all-gather.10
  152.7 17.6 all-gather.12
  171.8 17.6 all-gather.14
  191.1 17.6 all-gather.16
